TPU v7x, 32 devices: a whole 2x2x4 slice. The times are simulated.
32 devices in a mesh: rows: 4 (over x, core), cols: 8 (over z, y).
Axes of the slice: x: 2, y: 2, z: 4, core: 2. Of those that a mesh axis runs over, the one named last changes fastest.
Arguments:
- samples: bfloat16 [2048, 65536], P('rows', 'cols'), may hold values from -0.0234375 to 0.0234375
- labels: int32 [2048], P('rows'), may hold values 0 or 1
- weights: float32 [65536], P('cols'), may hold values from -7 to 7, as said below
- hist_s: float32 [16, 65536], P(None, 'cols'), may hold values from -60 to 60
- hist_y: float32 [16, 65536], P(None, 'cols'), may hold values from -480 to 480, as said below
- counter: int32 [1], replicated, may hold values from 0 to 4095
Outputs:
- new_weights: float32 [65536], P('cols')
- gradient: float32 [65536], P('cols')
Inputs may be any that keep to these rules, and one draw needn't show every extreme that they name: weights share a common direction with the rows of hist_s. Each entry of hist_y[j] is a positive multiple of the same entry of hist_s[j], so s_j . y_j > 0.
All inputs are finite; a program needn't handle non-finite values. No bound on the sum of `labels` on one device may be relied on, other than what follows from the above.
Results may differ from a plain program's by a relative error of at most 0.0013.
Values sent between devices are 32-bit elements; how exact they have to be, the bound alone decides.
A program may use at most 64 MiB of HBM per device.

v0:
```python
import jax
import jax.numpy as jnp
from jax import lax
from jax.sharding import PartitionSpec as P

HIST = 16


penalty = 4.0
step_length = 0.5
highest = lax.Precision.HIGHEST


def row_share(values):
    width = values.shape[-1] // lax.axis_size("rows")
    return lax.dynamic_slice_in_dim(values, lax.axis_index("rows") * width, width, values.ndim - 1)


def quad_form(left, matrix, right):
    return jnp.dot(left, jnp.dot(matrix, right, precision=highest), precision=highest)


def gram_recursion(gram, basis, newest):
    count = 2 * HIST + 1
    places = jnp.arange(count, dtype=jnp.int32)
    select_s = (places == newest).astype(jnp.float32)
    select_y = (places == newest + HIST).astype(jnp.float32)
    gamma = quad_form(select_s, gram, select_y) / quad_form(select_y, gram, select_y)
    weights_of = (places == 2 * HIST).astype(jnp.float32)
    coefs = []
    pairs = []
    for step in range(HIST):
        slot = (newest - step) % HIST
        pick_s = (places == slot).astype(jnp.float32)
        pick_y = (places == slot + HIST).astype(jnp.float32)
        rho = 1.0 / quad_form(pick_s, gram, pick_y)
        coef = rho * quad_form(pick_s, gram, weights_of)
        coefs.append(coef)
        pairs.append((pick_s, pick_y, rho))
        weights_of = weights_of - coef * pick_y
    result_of = gamma * weights_of
    for step in reversed(range(HIST)):
        pick_s, pick_y, rho = pairs[step]
        beta = rho * quad_form(pick_y, gram, result_of)
        result_of = result_of + (coefs[step] - beta) * pick_s
    return jnp.dot(result_of, basis, precision=highest)


def body(samples, labels, weights, hist_s, hist_y, counter):
    margin_part = jnp.dot(samples, weights.astype(jnp.bfloat16), preferred_element_type=jnp.float32)
    margin = lax.psum(margin_part, "cols")
    resid = (jax.nn.sigmoid(margin) - labels.astype(jnp.float32)).astype(jnp.bfloat16)
    total_part = jnp.dot(resid, samples, preferred_element_type=jnp.float32)
    newest = counter[0] % HIST
    total = lax.psum(total_part, "rows")
    gradient = weights + penalty * total
    basis = jnp.concatenate([hist_s, hist_y, gradient[None, :]], axis=0)
    narrow_basis = row_share(basis)
    gram_part = jnp.dot(
        narrow_basis, narrow_basis.T, precision=highest, preferred_element_type=jnp.float32
    )
    gram = lax.psum(gram_part, ("rows", "cols"))
    result = gram_recursion(gram, basis, newest)
    return (weights - step_length * result, gradient)


def solution(mesh):
    in_specs = (P("rows", "cols"), P("rows"), P("cols"), P(None, "cols"), P(None, "cols"), P())
    out_specs = (P("cols"), P("cols"))
    return jax.shard_map(body, mesh=mesh, in_specs=in_specs, out_specs=out_specs, check_vma=False)
```

profile of v0, /device:TPU:0, one launch (start us, length us, event | category | flops | bytes accessed | tf_op | source)
XLA Modules:
  0.0 156.2 jit_solution(8693725162735482173)
XLA Ops:
  0.6 0.8 convert_element_type.8
  1.4 5.6 %fusion.186 = f32[1,512]{1,0:T(1,128)S(1)} fusion(bf16[512,8192]{1,0:T(8,128)(2,1)} %param.6, bf16[8192,1]{0,1:T(2,128)(2,1)S(1)} %reshape.4), kind=kOutput, calls=%fused_computation.303 | convolution fusion | flops 8388608 | bytes 8407040 | tf_op jit(solution)/shard_map/dot_general | solution.py:50
  7.1 23.1 %psum.21 = f32[512]{0:T(512)S(1)} all-reduce(f32[512]{0:T(512)S(1)} %bitcast.507), channel_id=1, replica_groups=mesh['rows'=4,'cols'=8] {'cols'}, use_global_device_ids=true, to_apply=%region_0.0 | all-reduce | flops 512 | bytes 4096 | tf_op jit(solution)/shard_map/psum | solution.py:51
  30.3 4.7 %fusion.187 = f32[1,8192]{1,0:T(1,128)S(1)} fusion(bf16[512,1]{0,1:T(2,128)(2,1)S(1)} %reshape.6, bf16[512,8192]{1,0:T(8,128)(2,1)} %param.6), kind=kOutput, calls=%fused_computation.304 | convolution fusion | flops 8388608 | bytes 8422400 | tf_op jit(solution)/shard_map/dot_general | solution.py:53
  34.9 10.3 %psum.22 = f32[8192]{0:T(1024)S(1)} all-reduce(f32[8192]{0:T(1024)S(1)} %bitcast.505), channel_id=1, replica_groups=mesh['rows'=4,'cols'=8] {'rows'}, use_global_device_ids=true, to_apply=%region_1.2 | all-reduce | flops 8192 | bytes 65536 | tf_op jit(solution)/shard_map/psum | solution.py:55
  45.3 0.1 pad_maximum_fusion
  45.4 0.4 fusion.96
  45.8 37.1 %psum.23 = f32[33,33]{1,0:T(8,128)S(1)} all-reduce(f32[33,33]{1,0:T(8,128)S(1)} %fusion.96), channel_id=1, replica_groups=mesh['rows'=4,'cols'=8] {'rows','cols'}, use_global_device_ids=true, to_apply=%region_2.3 | all-reduce | flops 1089 | bytes 8712 | tf_op jit(solution)/shard_map/psum | solution.py:62
  83.6 0.7 fusion.48
  85.0 0.7 fusion.49
  86.5 0.7 fusion.50
  87.9 0.8 fusion.51
  89.3 0.7 fusion.52
  90.8 0.8 fusion.53
  92.2 0.7 fusion.56
  93.6 0.7 fusion.54
  95.1 0.8 fusion.55
  96.5 0.8 fusion.57
  97.9 0.7 fusion.60
  99.4 0.7 fusion.58
  100.8 0.8 fusion.59
  102.2 0.8 fusion.61
  103.7 0.7 fusion.64
  105.1 0.7 fusion.62
  106.6 0.8 fusion.63
  108.0 0.8 fusion.65
  109.4 0.7 fusion.68
  110.9 0.7 fusion.66
  112.3 0.8 fusion.67
  113.7 0.8 fusion.69
  115.2 0.7 fusion.72
  116.6 0.7 fusion.70
  118.1 0.8 fusion.71
  119.5 0.8 fusion.73
  120.9 0.7 fusion.76
  122.4 0.7 fusion.74
  123.8 0.8 fusion.75
  125.3 0.8 fusion.77
  126.7 0.7 fusion.78
  128.1 0.8 fusion.79
  129.5 0.8 fusion.121
  131.8 0.8 fusion.80
  133.2 0.8 fusion.81
  134.7 0.8 fusion.82
  136.1 0.8 fusion.83
  137.5 0.1 select_add_fusion.11
  137.6 0.8 fusion.84
  139.0 0.8 fusion.85
  140.4 0.1 select_add_fusion.9
  140.4 0.8 fusion.86
  141.9 0.8 fusion.87
  143.3 0.1 select_add_fusion.7
  143.3 0.8 fusion.88
  144.8 0.8 fusion.89
  146.2 0.1 select_add_fusion.5
  146.2 0.8 fusion.90
  147.6 0.8 fusion.91
  149.1 0.1 select_add_fusion.3
  149.1 0.8 fusion.92
  150.6 0.8 fusion.93
  152.0 0.8 fusion.94
  153.4 0.8 fusion.95
  154.8 0.7 fusion.124
  155.5 0.6 multiply_subtract_fusion
  (23 shorter events, 0.3 us)
Async XLA Ops:
  1.4 28.8 %copy-start.4 = (s32[512]{0:T(512)S(1)}, s32[512]{0:T(512)}, u32[]{:S(2)}) copy-start(s32[512]{0:T(512)} %param.7) | copy-start | bytes 6148
  30.2 15.0 %copy-start.2 = (f32[8192]{0:T(1024)S(1)}, f32[8192]{0:T(1024)}, u32[]{:S(2)}) copy-start(f32[8192]{0:T(1024)} %param.8) | copy-start | bytes 98308
  30.3 15.0 %copy-start = (f32[16,8192]{1,0:T(8,128)S(1)}, f32[16,8192]{1,0:T(8,128)}, u32[]{:S(2)}) copy-start(f32[16,8192]{1,0:T(8,128)} %param.10) | copy-start | bytes 1572868
  30.3 15.0 %copy-start.1 = (f32[16,8192]{1,0:T(8,128)S(1)}, f32[16,8192]{1,0:T(8,128)}, u32[]{:S(2)}) copy-start(f32[16,8192]{1,0:T(8,128)} %param.9) | copy-start | bytes 1572868
  45.2 109.5 %copy-start.3 = (f32[8192]{0:T(1024)}, f32[8192]{0:T(1024)S(1)}, u32[]{:S(2)}) copy-start(f32[8192]{0:T(1024)S(1)} %multiply_add_fusion) | copy-start | bytes 98308
where the time goes:
time: 158 us; the launch traced here: 156 us
  blocking collectives  70.5 us (45%)
  matrix products  48.3 us (31%)
  between operations  35.2 us (22%)
  other arithmetic  2.05 us (1%)
    psum x1, blocking collectives, body(): gram = lax.psum(gram_part, ('rows', 'cols'))  37.1 us
    dot_general x49, matrix products, quad_form(): jnp.dot(matrix, right, precision=highest)  36.8 us
    psum x1, blocking collectives, body(): margin = lax.psum(margin_part, 'cols')  23.1 us
    psum x1, blocking collectives, body(): total = lax.psum(total_part, 'rows')  10.3 us
    dot_general x1, matrix products, body(): jnp.dot(samples, weights.astype(jnp.bfloat16), preferred_element_type=jnp...  5.64 us
    dot_general x1, matrix products, body(): total_part = jnp.dot(resid, samples, preferred_element_type=jnp.float32)  4.66 us

commit v1 on v0

v1 whole, which is shorter than its diff:
```python
import functools

import jax
import jax.numpy as jnp
from jax import lax
from jax.experimental import pallas as pl
from jax.experimental.pallas import tpu as pltpu
from jax.sharding import PartitionSpec as P

HIST = 16
LANES = 128
LOAD_CHUNKS = 8
SEND_CHUNKS = 4

penalty = 4.0
step_length = 0.5
highest = lax.Precision.HIGHEST
f32 = jnp.float32
bf16 = jnp.bfloat16


def dot_nt(left, right, precision=None):
    return lax.dot_general(
        left, right, (((1,), (1,)), ((), ())), precision=precision, preferred_element_type=f32
    )


def split(values):
    high = values.astype(bf16)
    rest = values - high.astype(f32)
    return high, rest


def iota(shape, dim):
    return lax.broadcasted_iota(jnp.int32, shape, dim)


def kernel(
    rows, cols,
    counter_ref, labels_ref, samples_hbm, weights_hbm, s_hbm, y_hbm,
    out_ref, grad_ref,
    samples, weights, hist, basis, gram_slots, margin_slots, dot_slots, total_slots,
    load_sem, hist_sem, gram_send, gram_recv, margin_send, margin_recv,
    dot_send, dot_recv, total_send, total_recv,
):
    my_row, my_col = lax.axis_index("rows"), lax.axis_index("cols")
    count = rows * cols
    my_place = my_row * cols + my_col
    feat = samples.shape[1]
    wide = feat // LOAD_CHUNKS
    part = feat // SEND_CHUNKS

    first = [
        pltpu.make_async_copy(s_hbm, hist.at[pl.ds(0, HIST)], hist_sem.at[0]),
        pltpu.make_async_copy(y_hbm, hist.at[pl.ds(HIST, HIST)], hist_sem.at[1]),
        pltpu.make_async_copy(weights_hbm, weights, hist_sem.at[2]),
    ]
    loads = [
        pltpu.make_async_copy(
            samples_hbm.at[:, pl.ds(c * wide, wide)],
            samples.at[:, pl.ds(c * wide, wide)],
            load_sem.at[c],
        )
        for c in range(LOAD_CHUNKS)
    ]
    for copy in first + loads:
        copy.start()

    barrier = pltpu.get_barrier_semaphore()

    def greet(k, carry):
        place = lax.rem(my_place + k, count)
        pl.semaphore_signal(
            barrier, inc=1, device_id=(place // cols, lax.rem(place, cols)),
            device_id_type=pl.DeviceIdType.MESH,
        )
        return carry

    lax.fori_loop(1, count, greet, 0)

    for copy in first:
        copy.wait()
    for c in range(LOAD_CHUNKS):
        at = pl.ds(c * wide, wide)
        high, rest = split(hist[:, at])
        basis[0:32, at] = high
        basis[32:64, at] = rest.astype(bf16)
        w_high, w_rest = split(weights[:, at])
        w_mid, w_rest = split(w_rest)
        line = iota((16, wide), 0)
        block = jnp.where(line == 0, w_high.astype(f32), 0.0)
        block = jnp.where(line == 1, w_mid.astype(f32), block)
        block = jnp.where(line == 2, w_rest, block)
        basis[64:80, at] = block.astype(bf16)
        basis[80:128, at] = jnp.zeros((48, wide), bf16)

    gram = dot_nt(basis[0:80, :], basis[...])
    gram_y = gram[16:32] + gram[48:64]
    gram_y = gram_y + pltpu.roll(gram_y, LANES - 32, 1)
    w_line = jnp.sum(gram[64:80], axis=0, keepdims=True)
    w_line = w_line + pltpu.roll(w_line, LANES - 32, 1)
    gram_slots[my_col] = gram_y

    pl.semaphore_wait(barrier, count - 1)

    def over_cols(slots, send, recv):
        def copy_to(k):
            place = lax.rem(my_col + k, cols)
            return pltpu.make_async_remote_copy(
                src_ref=slots.at[my_col], dst_ref=slots.at[my_col],
                send_sem=send.at[k], recv_sem=recv.at[my_col],
                device_id=(my_row, place), device_id_type=pl.DeviceIdType.MESH,
            )

        def copy_from(k):
            place = lax.rem(my_col + k, cols)
            return pltpu.make_async_remote_copy(
                src_ref=slots.at[place], dst_ref=slots.at[place],
                send_sem=send.at[k], recv_sem=recv.at[place],
                device_id=(my_row, place), device_id_type=pl.DeviceIdType.MESH,
            )

        return copy_to, copy_from

    gram_to, gram_from = over_cols(gram_slots, gram_send, gram_recv)
    margin_to, margin_from = over_cols(margin_slots, margin_send, margin_recv)
    for k in range(1, cols):
        gram_to(k).start()

    product = None
    for c in range(LOAD_CHUNKS):
        at = pl.ds(c * wide, wide)
        loads[c].wait()
        term = dot_nt(basis[0:80, at], samples[:, at])
        product = term if product is None else product + term
    margin_slots[my_col] = product[64:65]
    for k in range(1, cols):
        margin_to(k).start()
    projected = product[0:32] + product[32:64]

    for k in range(1, cols):
        gram_from(k).wait_recv()
    gram = gram_slots[0]
    for k in range(1, cols):
        gram = gram + gram_slots[k]
    newest = lax.rem(counter_ref[0], HIST)
    line, lane = iota((HIST, LANES), 0), iota((HIST, LANES), 1)
    small = lane < HIST
    eye = line == lane
    age_line = lax.rem(newest - line + HIST, HIST)
    age_lane = lax.rem(newest - lane + LANES, HIST)
    sy = jnp.where(small, gram, 0.0)
    yy = jnp.where(small, pltpu.roll(gram, LANES - HIST, 1), 0.0)
    diagonal = jnp.where(eye, sy, 0.0)
    rho_line = 1.0 / jnp.sum(diagonal, axis=1, keepdims=True)
    diag_lane = jnp.sum(diagonal, axis=0, keepdims=True)
    rho_lane = 1.0 / jnp.where(small[0:1], diag_lane, 1.0)
    at_newest = jnp.logical_and(eye, line == newest)
    gamma = jnp.sum(
        jnp.sum(jnp.where(at_newest, sy, 0.0), axis=1, keepdims=True), axis=0, keepdims=True
    ) / jnp.sum(
        jnp.sum(jnp.where(at_newest, yy, 0.0), axis=1, keepdims=True), axis=0, keepdims=True
    )
    strict = jnp.logical_and(small, age_lane > age_line)
    factor = jnp.where(strict, sy * rho_lane, 0.0)
    solved = jnp.where(eye, 1.0, 0.0)
    columns = [
        jnp.sum(jnp.where(age_lane == age, factor, 0.0), axis=1, keepdims=True)
        for age in range(HIST)
    ]
    for age in reversed(range(1, HIST)):
        row = jnp.sum(jnp.where(age_line == age, solved, 0.0), axis=0, keepdims=True)
        solved = solved - columns[age] * row
    solved = solved * rho_line
    tall = lambda block: jnp.concatenate([block, jnp.zeros((LANES - HIST, LANES), f32)], axis=0)
    middle = diagonal + gamma * yy
    inverse = dot_nt(jnp.where(eye, 1.0, 0.0), tall(solved), highest)
    half = dot_nt(middle, tall(solved), highest)
    lower = jnp.dot(solved, tall(half), precision=highest, preferred_element_type=f32)
    map_y = -gamma * inverse
    map_s = lower - gamma * pltpu.roll(solved, HIST, 1)

    labels = labels_ref[...].astype(f32)
    for k in range(1, cols):
        margin_from(k).wait_recv()
    margin = margin_slots[0]
    for k in range(1, cols):
        margin = margin + margin_slots[k]
    resid = (jax.nn.sigmoid(margin) - labels).astype(bf16)
    resid_wide = resid.astype(f32)
    dots = jnp.sum(projected * resid_wide, axis=1, keepdims=True)
    spread = jnp.where(iota((32, LANES), 0) == iota((32, LANES), 1), dots, 0.0)
    dot_slots[my_place] = penalty * jnp.sum(spread, axis=0, keepdims=True) + w_line * (1.0 / rows)

    def dot_copy(k, owner):
        place = lax.rem(my_place + k, count)
        slot = my_place if owner else place
        return pltpu.make_async_remote_copy(
            src_ref=dot_slots.at[slot], dst_ref=dot_slots.at[slot],
            send_sem=dot_send.at[k], recv_sem=dot_recv.at[slot],
            device_id=(place // cols, lax.rem(place, cols)),
            device_id_type=pl.DeviceIdType.MESH,
        )

    def dot_start(k, carry):
        dot_copy(k, True).start()
        return carry

    lax.fori_loop(1, count, dot_start, 0)

    def total_copy(k, c, owner):
        place = lax.rem(my_row + k, rows)
        slot = my_row if owner else place
        return pltpu.make_async_remote_copy(
            src_ref=total_slots.at[slot, c], dst_ref=total_slots.at[slot, c],
            send_sem=total_send.at[k, c], recv_sem=total_recv.at[slot, c],
            device_id=(place, my_col), device_id_type=pl.DeviceIdType.MESH,
        )

    resid_rows = jnp.broadcast_to(resid_wide, (16, resid.shape[1])).astype(bf16)
    for c in range(SEND_CHUNKS):
        at = pl.ds(c * part, part)
        total = jnp.dot(resid_rows, samples[:, at], preferred_element_type=f32)
        total_slots[my_row, c] = total[0:1]
        for k in range(1, rows):
            total_copy(k, c, True).start()

    def dot_wait(k, carry):
        dot_copy(k, False).wait_recv()
        return carry

    lax.fori_loop(1, count, dot_wait, 0)
    inner = jnp.sum(dot_slots[...], axis=0)
    inner = jnp.where(iota((1, LANES), 1) < 32, inner, 0.0)
    coef_y = jnp.sum(map_y * inner, axis=1, keepdims=True)
    coef_s = jnp.sum(map_s * inner, axis=1, keepdims=True)
    for c in range(SEND_CHUNKS):
        at = pl.ds(c * part, part)
        mixed = jnp.sum(
            coef_s * hist[0:16, at] + coef_y * hist[16:32, at], axis=0, keepdims=True
        )
        for k in range(1, rows):
            total_copy(k, c, False).wait_recv()
        total = total_slots[0, c]
        for k in range(1, rows):
            total = total + total_slots[k, c]
        w = weights[:, at]
        gradient = w + penalty * total
        grad_ref[:, at] = gradient
        out_ref[:, at] = w - step_length * (gamma * gradient + mixed)

    for k in range(1, cols):
        gram_to(k).wait_send()
        margin_to(k).wait_send()

    def dot_sent(k, carry):
        dot_copy(k, True).wait_send()
        return carry

    lax.fori_loop(1, count, dot_sent, 0)
    for c in range(SEND_CHUNKS):
        for k in range(1, rows):
            total_copy(k, c, True).wait_send()


def body(rows, cols, samples, labels, weights, hist_s, hist_y, counter):
    height, feat = samples.shape
    count = rows * cols
    dma = pltpu.SemaphoreType.DMA
    anywhere = pl.BlockSpec(memory_space=pl.ANY)
    vmem = pl.BlockSpec(memory_space=pltpu.VMEM)
    new_weights, gradient = pl.pallas_call(
        functools.partial(kernel, rows, cols),
        out_shape=[jax.ShapeDtypeStruct((1, feat), f32)] * 2,
        in_specs=[pl.BlockSpec(memory_space=pltpu.SMEM), vmem] + [anywhere] * 4,
        out_specs=[vmem, vmem],
        scratch_shapes=[
            pltpu.VMEM((height, feat), bf16),
            pltpu.VMEM((1, feat), f32),
            pltpu.VMEM((2 * HIST, feat), f32),
            pltpu.VMEM((LANES, feat), bf16),
            pltpu.VMEM((cols, HIST, LANES), f32),
            pltpu.VMEM((cols, 1, height), f32),
            pltpu.VMEM((count, 1, LANES), f32),
            pltpu.VMEM((rows, SEND_CHUNKS, 1, feat // SEND_CHUNKS), f32),
            dma((LOAD_CHUNKS,)),
            dma((3,)),
            dma((cols,)),
            dma((cols,)),
            dma((cols,)),
            dma((cols,)),
            dma((count,)),
            dma((count,)),
            dma((rows, SEND_CHUNKS)),
            dma((rows, SEND_CHUNKS)),
        ],
        compiler_params=pltpu.CompilerParams(
            collective_id=0, has_side_effects=True, vmem_limit_bytes=60 * 1024 * 1024
        ),
    )(counter, labels.reshape(1, height), samples, weights.reshape(1, feat), hist_s, hist_y)
    return new_weights.reshape(feat), gradient.reshape(feat)


def solution(mesh):
    in_specs = (P("rows", "cols"), P("rows"), P("cols"), P(None, "cols"), P(None, "cols"), P())
    out_specs = (P("cols"), P("cols"))
    run = functools.partial(body, mesh.shape["rows"], mesh.shape["cols"])
    return jax.shard_map(run, mesh=mesh, in_specs=in_specs, out_specs=out_specs, check_vma=False)
```

time: 158 us -> 30.2 us (0.19)
  blocking collectives: 70.5 us -> 0 us
  matrix products: 48.3 us -> 0 us
  between operations: 35.2 us -> 1.29 us
  Pallas kernels: 0 us -> 25.8 us
  local copies, waits for them, and re-layouts: 0.06 us -> 2.75 us
  other arithmetic: 2.05 us -> 0 us
    psum x3 -> x0, blocking collectives: 70.5 us -> none  [the longest x1 37.1 us: body(): gram = lax.psum(gram_part, ('rows', 'cols'))]
    dot_general x53 -> x0, matrix products: 48.3 us -> none  [the longest x49 36.8 us: quad_form(): jnp.dot(matrix, right, precision=highest)]
    pallas_call x0 -> x1, Pallas kernels: none -> 25.8 us  [body(): pl.pallas_call(functools.partial(kernel, rows, cols), out_shape=[jax.Shap...]
    unnamed x10 -> x2, local copies, waits for them, and re-layouts: 0.03 us -> 2.75 us
where the time goes in v1:
time: 30.2 us; the launch traced here: 29.9 us
  Pallas kernels  25.8 us (85%)
  local copies, waits for them, and re-layouts  2.75 us (9%)
  between operations  1.29 us (4%)
    pallas_call x1, Pallas kernels, body(): pl.pallas_call(functools.partial(kernel, rows, cols), out_shape=[jax.Shap...  25.8 us
    unnamed x2, local copies, waits for them, and re-layouts  2.75 us

profile of v1, /device:TPU:0, one launch (start us, length us, event | category | flops | bytes accessed | tf_op | source)
XLA Modules:
  0.0 29.9 jit_solution(12055934181580049310)
XLA Ops:
  1.3 25.8 %shard_map.77 = (f32[1,8192]{1,0:T(1,128)}, f32[1,8192]{1,0:T(1,128)}) custom-call(s32[1]{0:T(128)S(6)} %copy.10.counter_ref, s32[1,512]{1,0:T(1,128)} %bitcast.7, bf16[512,8192]{1,0:T(8,128)(2,1)} %samples_hbm.1, f32[1,8192]{1,0:T(1,128)} %bitcast.4, f32[16,8192]{1,0:T(8,128)} %s_hbm.1, f32[16,8192]{1,0:T(8,128)} %y_hbm.1), custom_call_target="tpu_custom_call" | custom-call | tf_op jit(solution)/shard_map/pallas_call | solution.py:272
  27.1 1.4 %copy.11 = f32[8192]{0:T(1024)} copy(f32[8192]{0:T(1024)} %bitcast.6) | data formatting | bytes 65536
  28.5 1.4 %copy.12 = f32[8192]{0:T(1024)} copy(f32[8192]{0:T(1024)} %bitcast.5) | data formatting | bytes 65536

commit v2 on v1

--- a/solution.py
+++ b/solution.py
@@ -80,6 +80,29 @@
 
     for copy in first:
         copy.wait()
+
+    def over_cols(slots, send, recv):
+        def copy_to(k):
+            place = lax.rem(my_col + k, cols)
+            return pltpu.make_async_remote_copy(
+                src_ref=slots.at[my_col], dst_ref=slots.at[my_col],
+                send_sem=send.at[k], recv_sem=recv.at[my_col],
+                device_id=(my_row, place), device_id_type=pl.DeviceIdType.MESH,
+            )
+
+        def copy_from(k):
+            place = lax.rem(my_col + k, cols)
+            return pltpu.make_async_remote_copy(
+                src_ref=slots.at[place], dst_ref=slots.at[place],
+                send_sem=send.at[k], recv_sem=recv.at[place],
+                device_id=(my_row, place), device_id_type=pl.DeviceIdType.MESH,
+            )
+
+        return copy_to, copy_from
+
+    gram_to, gram_from = over_cols(gram_slots, gram_send, gram_recv)
+    margin_to, margin_from = over_cols(margin_slots, margin_send, margin_recv)
+    product = gram = None
     for c in range(LOAD_CHUNKS):
         at = pl.ds(c * wide, wide)
         high, rest = split(hist[:, at])
@@ -93,50 +116,68 @@
         block = jnp.where(line == 2, w_rest, block)
         basis[64:80, at] = block.astype(bf16)
         basis[80:128, at] = jnp.zeros((48, wide), bf16)
-
-    gram = dot_nt(basis[0:80, :], basis[...])
+        term = dot_nt(basis[0:80, at], basis[:, at])
+        gram = term if gram is None else gram + term
+        loads[c].wait()
+        term = dot_nt(basis[0:80, at], samples[:, at])
+        product = term if product is None else product + term
+    pl.semaphore_wait(barrier, count - 1)
+    margin_slots[my_col] = product[64:65]
+    for k in range(1, cols):
+        margin_to(k).start()
     gram_y = gram[16:32] + gram[48:64]
     gram_y = gram_y + pltpu.roll(gram_y, LANES - 32, 1)
     w_line = jnp.sum(gram[64:80], axis=0, keepdims=True)
     w_line = w_line + pltpu.roll(w_line, LANES - 32, 1)
     gram_slots[my_col] = gram_y
-
-    pl.semaphore_wait(barrier, count - 1)
-
-    def over_cols(slots, send, recv):
-        def copy_to(k):
-            place = lax.rem(my_col + k, cols)
-            return pltpu.make_async_remote_copy(
-                src_ref=slots.at[my_col], dst_ref=slots.at[my_col],
-                send_sem=send.at[k], recv_sem=recv.at[my_col],
-                device_id=(my_row, place), device_id_type=pl.DeviceIdType.MESH,
-            )
-
-        def copy_from(k):
-            place = lax.rem(my_col + k, cols)
-            return pltpu.make_async_remote_copy(
-                src_ref=slots.at[place], dst_ref=slots.at[place],
-                send_sem=send.at[k], recv_sem=recv.at[place],
-                device_id=(my_row, place), device_id_type=pl.DeviceIdType.MESH,
-            )
-
-        return copy_to, copy_from
-
-    gram_to, gram_from = over_cols(gram_slots, gram_send, gram_recv)
-    margin_to, margin_from = over_cols(margin_slots, margin_send, margin_recv)
     for k in range(1, cols):
         gram_to(k).start()
-
-    product = None
-    for c in range(LOAD_CHUNKS):
-        at = pl.ds(c * wide, wide)
-        loads[c].wait()
-        term = dot_nt(basis[0:80, at], samples[:, at])
-        product = term if product is None else product + term
-    margin_slots[my_col] = product[64:65]
-    for k in range(1, cols):
-        margin_to(k).start()
     projected = product[0:32] + product[32:64]
+
+    labels = labels_ref[...].astype(f32)
+    for k in range(1, cols):
+        margin_from(k).wait_recv()
+    margin = margin_slots[0]
+    for k in range(1, cols):
+        margin = margin + margin_slots[k]
+    resid = (jax.nn.sigmoid(margin) - labels).astype(bf16)
+    resid_wide = resid.astype(f32)
+    dots = jnp.sum(projected * resid_wide, axis=1, keepdims=True)
+    spread = jnp.where(iota((32, LANES), 0) == iota((32, LANES), 1), dots, 0.0)
+    dot_slots[my_place] = penalty * jnp.sum(spread, axis=0, keepdims=True) + w_line * (1.0 / rows)
+
+    def dot_copy(k, owner):
+        place = lax.rem(my_place + k, count)
+        slot = my_place if owner else place
+        return pltpu.make_async_remote_copy(
+            src_ref=dot_slots.at[slot], dst_ref=dot_slots.at[slot],
+            send_sem=dot_send.at[k], recv_sem=dot_recv.at[slot],
+            device_id=(place // cols, lax.rem(place, cols)),
+            device_id_type=pl.DeviceIdType.MESH,
+        )
+
+    def dot_start(k, carry):
+        dot_copy(k, True).start()
+        return carry
+
+    lax.fori_loop(1, count, dot_start, 0)
+
+    def total_copy(k, c, owner):
+        place = lax.rem(my_row + k, rows)
+        slot = my_row if owner else place
+        return pltpu.make_async_remote_copy(
+            src_ref=total_slots.at[slot, c], dst_ref=total_slots.at[slot, c],
+            send_sem=total_send.at[k, c], recv_sem=total_recv.at[slot, c],
+            device_id=(place, my_col), device_id_type=pl.DeviceIdType.MESH,
+        )
+
+    resid_rows = jnp.broadcast_to(resid_wide, (16, resid.shape[1])).astype(bf16)
+    for c in range(SEND_CHUNKS):
+        at = pl.ds(c * part, part)
+        total = jnp.dot(resid_rows, samples[:, at], preferred_element_type=f32)
+        total_slots[my_row, c] = total[0:1]
+        for k in range(1, rows):
+            total_copy(k, c, True).start()
 
     for k in range(1, cols):
         gram_from(k).wait_recv()
@@ -180,51 +221,6 @@
     map_y = -gamma * inverse
     map_s = lower - gamma * pltpu.roll(solved, HIST, 1)
 
-    labels = labels_ref[...].astype(f32)
-    for k in range(1, cols):
-        margin_from(k).wait_recv()
-    margin = margin_slots[0]
-    for k in range(1, cols):
-        margin = margin + margin_slots[k]
-    resid = (jax.nn.sigmoid(margin) - labels).astype(bf16)
-    resid_wide = resid.astype(f32)
-    dots = jnp.sum(projected * resid_wide, axis=1, keepdims=True)
-    spread = jnp.where(iota((32, LANES), 0) == iota((32, LANES), 1), dots, 0.0)
-    dot_slots[my_place] = penalty * jnp.sum(spread, axis=0, keepdims=True) + w_line * (1.0 / rows)
-
-    def dot_copy(k, owner):
-        place = lax.rem(my_place + k, count)
-        slot = my_place if owner else place
-        return pltpu.make_async_remote_copy(
-            src_ref=dot_slots.at[slot], dst_ref=dot_slots.at[slot],
-            send_sem=dot_send.at[k], recv_sem=dot_recv.at[slot],
-            device_id=(place // cols, lax.rem(place, cols)),
-            device_id_type=pl.DeviceIdType.MESH,
-        )
-
-    def dot_start(k, carry):
-        dot_copy(k, True).start()
-        return carry
-
-    lax.fori_loop(1, count, dot_start, 0)
-
-    def total_copy(k, c, owner):
-        place = lax.rem(my_row + k, rows)
-        slot = my_row if owner else place
-        return pltpu.make_async_remote_copy(
-            src_ref=total_slots.at[slot, c], dst_ref=total_slots.at[slot, c],
-            send_sem=total_send.at[k, c], recv_sem=total_recv.at[slot, c],
-            device_id=(place, my_col), device_id_type=pl.DeviceIdType.MESH,
-        )
-
-    resid_rows = jnp.broadcast_to(resid_wide, (16, resid.shape[1])).astype(bf16)
-    for c in range(SEND_CHUNKS):
-        at = pl.ds(c * part, part)
-        total = jnp.dot(resid_rows, samples[:, at], preferred_element_type=f32)
-        total_slots[my_row, c] = total[0:1]
-        for k in range(1, rows):
-            total_copy(k, c, True).start()
-
     def dot_wait(k, carry):
         dot_copy(k, False).wait_recv()
         return carry
@@ -244,10 +240,9 @@
         total = total_slots[0, c]
         for k in range(1, rows):
             total = total + total_slots[k, c]
-        w = weights[:, at]
-        gradient = w + penalty * total
-        grad_ref[:, at] = gradient
-        out_ref[:, at] = w - step_length * (gamma * gradient + mixed)
+        total = penalty * total
+        grad_ref[:, at] = total
+        out_ref[:, at] = -step_length * (gamma * (weights[:, at] + total) + mixed)
 
     for k in range(1, cols):
         gram_to(k).wait_send()
@@ -269,7 +264,7 @@
     dma = pltpu.SemaphoreType.DMA
     anywhere = pl.BlockSpec(memory_space=pl.ANY)
     vmem = pl.BlockSpec(memory_space=pltpu.VMEM)
-    new_weights, gradient = pl.pallas_call(
+    direction, total = pl.pallas_call(
         functools.partial(kernel, rows, cols),
         out_shape=[jax.ShapeDtypeStruct((1, feat), f32)] * 2,
         in_specs=[pl.BlockSpec(memory_space=pltpu.SMEM), vmem] + [anywhere] * 4,
@@ -298,7 +293,8 @@
             collective_id=0, has_side_effects=True, vmem_limit_bytes=60 * 1024 * 1024
         ),
     )(counter, labels.reshape(1, height), samples, weights.reshape(1, feat), hist_s, hist_y)
-    return new_weights.reshape(feat), gradient.reshape(feat)
+    direction, total = direction.reshape(feat), total.reshape(feat)
+    return weights + direction, weights + total
 
 
 def solution(mesh):

time: 30.2 us -> 27.3 us (0.904)
  local copies, waits for them, and re-layouts: 2.75 us -> 0.01 us
  Pallas kernels: 25.8 us -> 24.3 us
  other arithmetic: 0 us -> 1.41 us
    unnamed x2, local copies, waits for them, and re-layouts: 2.75 us -> 0.01 us
    pallas_call x1, Pallas kernels: 25.8 us -> 24.3 us  [body(): pl.pallas_call(functools.partial(kernel, rows, cols), out_shape=[jax.Shap...]
    add x0 -> x1, other arithmetic: none -> 1.41 us  [body(): return (weights + direction, weights + total)]
where the time goes in v2:
time: 27.3 us; the launch traced here: 27 us
  Pallas kernels  24.3 us (89%)
  other arithmetic  1.41 us (5%)
  between operations  1.31 us (5%)
    pallas_call x1, Pallas kernels, body(): pl.pallas_call(functools.partial(kernel, rows, cols), out_shape=[jax.Shap...  24.3 us
    add x1, other arithmetic, body(): return (weights + direction, weights + total)  1.41 us

profile of v2, /device:TPU:0, one launch (start us, length us, event | category | flops | bytes accessed | tf_op | source)
XLA Modules:
  0.0 27.0 jit_solution(1711024545504623368)
XLA Ops:
  0.6 0.0 copy-start
  1.3 24.3 %shard_map.77 = (f32[1,8192]{1,0:T(1,128)}, f32[1,8192]{1,0:T(1,128)}) custom-call(s32[1]{0:T(128)S(6)} %copy.8.counter_ref, s32[1,512]{1,0:T(1,128)} %bitcast.7, bf16[512,8192]{1,0:T(8,128)(2,1)} %samples_hbm.1, f32[1,8192]{1,0:T(1,128)} %bitcast.4, f32[16,8192]{1,0:T(8,128)} %s_hbm.1, f32[16,8192]{1,0:T(8,128)} %y_hbm.1), custom_call_target="tpu_custom_call" | custom-call | tf_op jit(solution)/shard_map/pallas_call | solution.py:267
  25.6 0.0 copy-done
  25.6 1.4 %fusion = (f32[8192]{0:T(1024)}, f32[8192]{0:T(1024)}) fusion(f32[8192]{0:T(1024)S(1)} %copy-done, f32[8192]{0:T(1024)} %bitcast.6, f32[8192]{0:T(1024)} %bitcast.5), kind=kLoop, calls=%fused_computation | loop fusion | flops 16384 | bytes 163840 | tf_op jit(solution)/shard_map/add | solution.py:297
Async XLA Ops:
  0.6 24.9 %copy-start = (f32[8192]{0:T(1024)S(1)}, f32[8192]{0:T(1024)}, u32[]{:S(2)}) copy-start(f32[8192]{0:T(1024)} %param.8) | copy-start | bytes 98308

commit v3 on v2

--- a/solution.py
+++ b/solution.py
@@ -9,7 +9,7 @@
 
 HIST = 16
 LANES = 128
-LOAD_CHUNKS = 8
+LOAD_CHUNKS = 16
 SEND_CHUNKS = 4
 
 penalty = 4.0
@@ -37,9 +37,9 @@
 
 def kernel(
     rows, cols,
-    counter_ref, labels_ref, samples_hbm, weights_hbm, s_hbm, y_hbm,
+    counter_ref, labels_hbm, samples_hbm, weights_hbm, s_hbm, y_hbm,
     out_ref, grad_ref,
-    samples, weights, hist, basis, gram_slots, margin_slots, dot_slots, total_slots,
+    labels_ref, samples, weights, hist, basis, gram_slots, margin_slots, dot_slots, total_slots,
     load_sem, hist_sem, gram_send, gram_recv, margin_send, margin_recv,
     dot_send, dot_recv, total_send, total_recv,
 ):
@@ -63,7 +63,8 @@
         )
         for c in range(LOAD_CHUNKS)
     ]
-    for copy in first + loads:
+    label_copy = pltpu.make_async_copy(labels_hbm, labels_ref, hist_sem.at[3])
+    for copy in first + loads + [label_copy]:
         copy.start()
 
     barrier = pltpu.get_barrier_semaphore()
@@ -102,7 +103,7 @@
 
     gram_to, gram_from = over_cols(gram_slots, gram_send, gram_recv)
     margin_to, margin_from = over_cols(margin_slots, margin_send, margin_recv)
-    product = gram = None
+    product = None
     for c in range(LOAD_CHUNKS):
         at = pl.ds(c * wide, wide)
         high, rest = split(hist[:, at])
@@ -116,8 +117,6 @@
         block = jnp.where(line == 2, w_rest, block)
         basis[64:80, at] = block.astype(bf16)
         basis[80:128, at] = jnp.zeros((48, wide), bf16)
-        term = dot_nt(basis[0:80, at], basis[:, at])
-        gram = term if gram is None else gram + term
         loads[c].wait()
         term = dot_nt(basis[0:80, at], samples[:, at])
         product = term if product is None else product + term
@@ -125,6 +124,7 @@
     margin_slots[my_col] = product[64:65]
     for k in range(1, cols):
         margin_to(k).start()
+    gram = dot_nt(basis[0:80, :], basis[...])
     gram_y = gram[16:32] + gram[48:64]
     gram_y = gram_y + pltpu.roll(gram_y, LANES - 32, 1)
     w_line = jnp.sum(gram[64:80], axis=0, keepdims=True)
@@ -134,6 +134,7 @@
         gram_to(k).start()
     projected = product[0:32] + product[32:64]
 
+    label_copy.wait()
     labels = labels_ref[...].astype(f32)
     for k in range(1, cols):
         margin_from(k).wait_recv()
@@ -156,11 +157,15 @@
             device_id_type=pl.DeviceIdType.MESH,
         )
 
-    def dot_start(k, carry):
-        dot_copy(k, True).start()
-        return carry
-
-    lax.fori_loop(1, count, dot_start, 0)
+    for i in range(rows):
+        for j in range(cols):
+            if i or j:
+                pltpu.make_async_remote_copy(
+                    src_ref=dot_slots.at[my_place], dst_ref=dot_slots.at[my_place],
+                    send_sem=dot_send.at[i * cols + j], recv_sem=dot_recv.at[my_place],
+                    device_id=(lax.rem(my_row + i, rows), lax.rem(my_col + j, cols)),
+                    device_id_type=pl.DeviceIdType.MESH,
+                ).start()
 
     def total_copy(k, c, owner):
         place = lax.rem(my_row + k, rows)
@@ -228,6 +233,15 @@
     lax.fori_loop(1, count, dot_wait, 0)
     inner = jnp.sum(dot_slots[...], axis=0)
     inner = jnp.where(iota((1, LANES), 1) < 32, inner, 0.0)
+    for k in range(1, cols):
+        gram_to(k).wait_send()
+        margin_to(k).wait_send()
+
+    def dot_sent(k, carry):
+        dot_copy(k, True).wait_send()
+        return carry
+
+    lax.fori_loop(1, count, dot_sent, 0)
     coef_y = jnp.sum(map_y * inner, axis=1, keepdims=True)
     coef_s = jnp.sum(map_s * inner, axis=1, keepdims=True)
     for c in range(SEND_CHUNKS):
@@ -244,15 +258,6 @@
         grad_ref[:, at] = total
         out_ref[:, at] = -step_length * (gamma * (weights[:, at] + total) + mixed)
 
-    for k in range(1, cols):
-        gram_to(k).wait_send()
-        margin_to(k).wait_send()
-
-    def dot_sent(k, carry):
-        dot_copy(k, True).wait_send()
-        return carry
-
-    lax.fori_loop(1, count, dot_sent, 0)
     for c in range(SEND_CHUNKS):
         for k in range(1, rows):
             total_copy(k, c, True).wait_send()
@@ -267,9 +272,10 @@
     direction, total = pl.pallas_call(
         functools.partial(kernel, rows, cols),
         out_shape=[jax.ShapeDtypeStruct((1, feat), f32)] * 2,
-        in_specs=[pl.BlockSpec(memory_space=pltpu.SMEM), vmem] + [anywhere] * 4,
+        in_specs=[pl.BlockSpec(memory_space=pltpu.SMEM)] + [anywhere] * 5,
         out_specs=[vmem, vmem],
         scratch_shapes=[
+            pltpu.VMEM((1, height), jnp.int32),
             pltpu.VMEM((height, feat), bf16),
             pltpu.VMEM((1, feat), f32),
             pltpu.VMEM((2 * HIST, feat), f32),
@@ -279,7 +285,7 @@
             pltpu.VMEM((count, 1, LANES), f32),
             pltpu.VMEM((rows, SEND_CHUNKS, 1, feat // SEND_CHUNKS), f32),
             dma((LOAD_CHUNKS,)),
-            dma((3,)),
+            dma((4,)),
             dma((cols,)),
             dma((cols,)),
             dma((cols,)),

time: 27.3 us -> 25.6 us (0.938)
  Pallas kernels: 24.3 us -> 22.6 us
    pallas_call x1, Pallas kernels: 24.3 us -> 22.6 us  [body(): pl.pallas_call(functools.partial(kernel, rows, cols), out_shape=[jax.Shap...]
where the time goes in v3:
time: 25.6 us; the launch traced here: 25.4 us
  Pallas kernels  22.6 us (88%)
  other arithmetic  1.41 us (6%)
  between operations  1.31 us (5%)
    pallas_call x1, Pallas kernels, body(): pl.pallas_call(functools.partial(kernel, rows, cols), out_shape=[jax.Shap...  22.6 us
    add x1, other arithmetic, body(): return (weights + direction, weights + total)  1.41 us

profile of v3, /device:TPU:0, one launch (start us, length us, event | category | flops | bytes accessed | tf_op | source)
XLA Modules:
  0.0 25.4 jit_solution(7239251466695974889)
XLA Ops:
  0.6 0.0 copy-start
  1.3 22.6 %shard_map.77 = (f32[1,8192]{1,0:T(1,128)}, f32[1,8192]{1,0:T(1,128)}) custom-call(s32[1]{0:T(128)S(6)} %copy.8.counter_ref, s32[1,512]{1,0:T(1,128)} %bitcast.7, bf16[512,8192]{1,0:T(8,128)(2,1)} %samples_hbm.1, f32[1,8192]{1,0:T(1,128)} %bitcast.4, f32[16,8192]{1,0:T(8,128)} %s_hbm.1, f32[16,8192]{1,0:T(8,128)} %y_hbm.1), custom_call_target="tpu_custom_call" | custom-call | tf_op jit(solution)/shard_map/pallas_call | solution.py:272
  23.9 0.0 copy-done
  23.9 1.4 %fusion = (f32[8192]{0:T(1024)}, f32[8192]{0:T(1024)}) fusion(f32[8192]{0:T(1024)S(1)} %copy-done, f32[8192]{0:T(1024)} %bitcast.6, f32[8192]{0:T(1024)} %bitcast.5), kind=kLoop, calls=%fused_computation | loop fusion | flops 16384 | bytes 163840 | tf_op jit(solution)/shard_map/add | solution.py:303
Async XLA Ops:
  0.6 23.3 %copy-start = (f32[8192]{0:T(1024)S(1)}, f32[8192]{0:T(1024)}, u32[]{:S(2)}) copy-start(f32[8192]{0:T(1024)} %param.8) | copy-start | bytes 98308
